TPU v7x, 128 devices: a whole 4x4x4 slice. The times are simulated.
128 devices in a mesh: row: 16 (over x_hi, z, core), col: 8 (over x_lo, y).
Axes of the slice: x: 4 (x_hi: 2, x_lo: 2; x = x_hi * 2 + x_lo), y: 4, z: 4, core: 2. Of those that a mesh axis runs over, the one named last changes fastest.
Arguments:
- local_inverse: float32 [1024, 512, 512], P(('row', 'col')), may hold values from -1 to 3.5, as said below
- coupling: float32 [1024, 512, 1024], P(('row', 'col')), may hold values from -0.03125 to 0.03125
- local_rhs: float32 [1024, 512], P(('row', 'col')), may hold values from -6 to 6
- members: int32 [1024, 8], P(('row', 'col')), may hold values from 0 to 15, all different within a row
- shared_matrix: float32 [2048, 2048], P('row', 'col'), may hold values from -2 to 66, as said below
- shared_rhs: float32 [2048], P('row'), may hold values from -6 to 6
- prior_solution: float32 [2048], P('row'), may hold values from -6 to 6
- preconditioner: float32 [2048], P('row'), may hold values from 0.008 to 0.02
Outputs:
- reduced_matrix: float32 [2048, 2048], P('row', 'col')
- reduced_rhs: float32 [2048], P('row')
- solution: float32 [2048], P('row')
Inputs may be any that keep to these rules, and one draw needn't show every extreme that they name: `members`: each week names 8 different station blocks. `local_inverse`: symmetric for every week. `shared_matrix`: symmetric.
All inputs are finite; a program needn't handle non-finite values.
Results may differ from a plain program's by a relative error of at most 0.00016.
Values sent between devices are 32-bit elements; how exact they have to be, the bound alone decides.
A program may use at most 256 MiB of HBM per device.

v0:
```python
import functools

import jax
import jax.numpy as jnp
from jax import lax
from jax.sharding import Mesh
from jax.sharding import PartitionSpec as P

BLOCK = 128
BLOCKS = 16
TOUCHED = 8
ITERS = 2
COL = ("col_0", "col_1")
ROW_COL = ("row", "col_0", "col_1")


highest = lax.Precision.HIGHEST


def split_up(shard, dim, count):
    dims = shard.shape
    tiles = shard.reshape(*dims[:dim], count, dims[dim] // count, *dims[dim + 1 :])
    return jnp.moveaxis(tiles, dim, 0)


def summed_on_arrival(shard, axis, dim):
    count = lax.axis_size(axis)
    tiles = lax.all_to_all(split_up(shard, dim, count), axis, 0, 0, tiled=True)
    return jnp.sum(tiles, axis=0)


def copy_for_each(shard, axis):
    count = lax.axis_size(axis)
    return lax.all_to_all(
        jnp.broadcast_to(shard[None], (count, *shard.shape)), axis, 0, 0, tiled=True
    )


def taken_together(shard, axis):
    return copy_for_each(shard, axis).sum(axis=0)


def over_axes(shard, axes):
    return functools.reduce(lax.psum, axes, shard)


def local(
    local_inverse,
    coupling,
    local_rhs,
    members,
    shared_matrix,
    shared_rhs,
    prior_solution,
    preconditioner,
):
    row_count = lax.axis_size("row")
    column_count = lax.axis_size(COL)
    row_blocks = BLOCKS // row_count
    column_blocks = BLOCKS // column_count
    tile_rows, tile_columns = shared_matrix.shape
    summed_grid = jnp.zeros(
        (row_count, column_count, row_blocks, column_blocks, BLOCK, BLOCK), jnp.float32
    )
    rhs_grid = jnp.zeros((row_count, row_blocks, BLOCK), jnp.float32)
    for week_index in range(local_inverse.shape[0]):
        coupling_week = coupling[week_index]
        mapped = jnp.dot(
            local_inverse[week_index],
            coupling_week,
            precision=highest,
            preferred_element_type=jnp.float32,
        )
        contribution = lax.dot_general(
            coupling_week,
            mapped,
            (((0,), (0,)), ((), ())),
            precision=highest,
            preferred_element_type=jnp.float32,
        )
        pushed = jnp.dot(
            local_rhs[week_index], mapped, precision=highest, preferred_element_type=jnp.float32
        )
        tile_grid = contribution.reshape(TOUCHED, BLOCK, TOUCHED, BLOCK).transpose(0, 2, 1, 3)
        blocks = members[week_index]
        row_owner = (blocks // row_blocks)[:, None]
        row_place = (blocks % row_blocks)[:, None]
        column_owner = (blocks // column_blocks)[None, :]
        column_place = (blocks % column_blocks)[None, :]
        summed_grid = summed_grid.at[row_owner, column_owner, row_place, column_place].add(
            tile_grid
        )
        rhs_grid = rhs_grid.at[blocks // row_blocks, blocks % row_blocks].add(
            pushed.reshape(TOUCHED, BLOCK)
        )
    row_grid, row_rhs = (
        lax.psum_scatter(summed_grid, "row", scatter_dimension=0, tiled=True),
        lax.psum_scatter(rhs_grid, "row", scatter_dimension=0, tiled=True),
    )
    owned = summed_on_arrival(row_grid, COL, 1)
    own_rhs = taken_together(row_rhs, COL)
    own_tile = (
        owned.reshape(row_blocks, column_blocks, BLOCK, BLOCK)
        .transpose(0, 2, 1, 3)
        .reshape(tile_rows, tile_columns)
    )
    reduced_matrix = shared_matrix - own_tile
    reduced_rhs = shared_rhs - own_rhs.reshape(tile_rows)
    solution = prior_solution
    column_start = lax.axis_index(COL) * tile_columns
    for iteration in range(ITERS):
        whole_iterate = lax.all_gather(solution, "row", axis=0, tiled=True)
        column_part = lax.dynamic_slice_in_dim(whole_iterate, column_start, tile_columns)
        row_product = jnp.dot(
            reduced_matrix, column_part, precision=highest, preferred_element_type=jnp.float32
        )
        product = over_axes(row_product, COL)
        solution = solution + preconditioner * (reduced_rhs - product)
    return (reduced_matrix, reduced_rhs, solution)


def solution(mesh):
    finer = Mesh(mesh.devices.reshape(mesh.shape["row"], 2, 4), ("row", "col_0", "col_1"))
    placed = (
        P(ROW_COL, None, None),
        P(ROW_COL, None, None),
        P(ROW_COL, None),
        P(ROW_COL, None),
        P("row", COL),
        P("row"),
        P("row"),
        P("row"),
    )
    return jax.shard_map(
        local,
        mesh=finer,
        in_specs=placed,
        out_specs=(P("row", COL), P("row"), P("row")),
        check_vma=False,
    )
```

profile of v0, /device:TPU:40, one launch (start us, length us, event | category | flops | bytes accessed | tf_op | source)
XLA Modules:
  0.0 564.5 jit_solution(6128873195023299404)
XLA Ops:
  60.4 9.0 %convolution_bitcast_fusion.7 = f32[128,8,8,128]{3,1,2,0:T(8,128)S(1)} fusion(f32[512,1024]{1,0:T(8,128)} %fusion.22, f32[8,512,1024]{2,1,0:T(8,128)} %param.9), kind=kOutput, calls=%fused_computation.23 | convolution fusion | flops 6442450944 | bytes 8388608 | tf_op jit(solution)/shard_map/dot_general | solution.py:74
  78.2 9.0 %convolution_bitcast_fusion.6 = f32[128,8,8,128]{3,1,2,0:T(8,128)S(1)} fusion(f32[512,1024]{1,0:T(8,128)} %fusion.19, f32[8,512,1024]{2,1,0:T(8,128)} %param.9), kind=kOutput, calls=%fused_computation.22 | convolution fusion | flops 6442450944 | bytes 8388608 | tf_op jit(solution)/shard_map/dot_general | solution.py:74
  95.9 9.0 %convolution_bitcast_fusion.5 = f32[128,8,8,128]{3,1,2,0:T(8,128)S(1)} fusion(f32[512,1024]{1,0:T(8,128)} %fusion.16, f32[8,512,1024]{2,1,0:T(8,128)} %param.9), kind=kOutput, calls=%fused_computation.21 | convolution fusion | flops 6442450944 | bytes 8388608 | tf_op jit(solution)/shard_map/dot_general | solution.py:74
  113.5 9.0 %convolution_bitcast_fusion.4 = f32[128,8,8,128]{3,1,2,0:T(8,128)S(1)} fusion(f32[512,1024]{1,0:T(8,128)} %fusion.13, f32[8,512,1024]{2,1,0:T(8,128)} %param.9), kind=kOutput, calls=%fused_computation.20 | convolution fusion | flops 6442450944 | bytes 8388608 | tf_op jit(solution)/shard_map/dot_general | solution.py:74
  131.3 9.0 %convolution_bitcast_fusion.3 = f32[128,8,8,128]{3,1,2,0:T(8,128)S(1)} fusion(f32[512,1024]{1,0:T(8,128)} %fusion.10, f32[8,512,1024]{2,1,0:T(8,128)} %param.9), kind=kOutput, calls=%fused_computation.19 | convolution fusion | flops 6442450944 | bytes 8388608 | tf_op jit(solution)/shard_map/dot_general | solution.py:74
  149.2 9.0 %convolution_bitcast_fusion.2 = f32[128,8,8,128]{3,1,2,0:T(8,128)S(1)} fusion(f32[512,1024]{1,0:T(8,128)} %fusion.7, f32[8,512,1024]{2,1,0:T(8,128)} %param.9), kind=kOutput, calls=%fused_computation.18 | convolution fusion | flops 6442450944 | bytes 8388608 | tf_op jit(solution)/shard_map/dot_general | solution.py:74
  166.9 9.0 %convolution_bitcast_fusion.1 = f32[128,8,8,128]{3,1,2,0:T(8,128)S(1)} fusion(f32[512,1024]{1,0:T(8,128)} %fusion.4, f32[8,512,1024]{2,1,0:T(8,128)} %param.9), kind=kOutput, calls=%fused_computation.17 | convolution fusion | flops 6442450944 | bytes 8388608 | tf_op jit(solution)/shard_map/dot_general | solution.py:74
  184.4 8.4 %convolution_bitcast_fusion = f32[128,8,8,128]{3,1,2,0:T(8,128)S(1)} fusion(f32[512,1024]{1,0:T(8,128)S(1)} %fusion.1, f32[8,512,1024]{2,1,0:T(8,128)} %param.9), kind=kOutput, calls=%fused_computation.16 | convolution fusion | flops 6442450944 | bytes 8388608 | tf_op jit(solution)/shard_map/dot_general | solution.py:74
  201.0 7.8 %broadcast.1276 = f32[16,8,2,128,128]{4,3,2,1,0:T(8,128)} broadcast(f32[]{:T(128)} %constant.307.clone.1), dimensions={} | broadcast | bytes 16777220 | tf_op jit(solution)/shard_map/broadcast_in_dim | solution.py:62
  208.9 14.5 %scatter_fusion = f32[16,8,2,128,128]{4,3,2,1,0:T(8,128)} fusion(f32[16,8,2,128,128]{4,3,2,1,0:T(8,128)} %broadcast.1276, s32[64]{0:T(128)S(1)} %reshape.560, f32[64,128,128]{2,1,0:T(8,128)} %bitcast.412), kind=kCustom, calls=%fused_computation | custom fusion | flops 1048576 | bytes 12583680 | tf_op jit(solution)/shard_map/scatter-add | solution.py:90
  223.3 14.5 %scatter_fusion.1 = f32[16,8,2,128,128]{4,3,2,1,0:T(8,128)} fusion(f32[16,8,2,128,128]{4,3,2,1,0:T(8,128)} %scatter_fusion, s32[64]{0:T(128)S(1)} %reshape.568, f32[64,128,128]{2,1,0:T(8,128)} %bitcast.413), kind=kCustom, calls=%fused_computation.1 | custom fusion | flops 1048576 | bytes 12583680 | tf_op jit(solution)/shard_map/scatter-add | solution.py:90
  237.9 14.9 %scatter_fusion.2 = f32[16,8,2,128,128]{4,3,2,1,0:T(8,128)} fusion(f32[16,8,2,128,128]{4,3,2,1,0:T(8,128)} %scatter_fusion.1, s32[64]{0:T(128)S(1)} %reshape.576, f32[64,128,128]{2,1,0:T(8,128)} %bitcast.414), kind=kCustom, calls=%fused_computation.2 | custom fusion | flops 1048576 | bytes 12583680 | tf_op jit(solution)/shard_map/scatter-add | solution.py:90
  252.8 14.4 %scatter_fusion.3 = f32[16,8,2,128,128]{4,3,2,1,0:T(8,128)} fusion(f32[16,8,2,128,128]{4,3,2,1,0:T(8,128)} %scatter_fusion.2, s32[64]{0:T(128)S(1)} %reshape.584, f32[64,128,128]{2,1,0:T(8,128)} %bitcast.415), kind=kCustom, calls=%fused_computation.3 | custom fusion | flops 1048576 | bytes 12583680 | tf_op jit(solution)/shard_map/scatter-add | solution.py:90
  267.2 14.5 %scatter_fusion.4 = f32[16,8,2,128,128]{4,3,2,1,0:T(8,128)} fusion(f32[16,8,2,128,128]{4,3,2,1,0:T(8,128)} %scatter_fusion.3, s32[64]{0:T(128)S(1)} %reshape.592, f32[64,128,128]{2,1,0:T(8,128)} %bitcast.416), kind=kCustom, calls=%fused_computation.4 | custom fusion | flops 1048576 | bytes 12583680 | tf_op jit(solution)/shard_map/scatter-add | solution.py:90
  281.8 14.5 %scatter_fusion.5 = f32[16,8,2,128,128]{4,3,2,1,0:T(8,128)} fusion(f32[16,8,2,128,128]{4,3,2,1,0:T(8,128)} %scatter_fusion.4, s32[64]{0:T(128)S(1)} %reshape.600, f32[64,128,128]{2,1,0:T(8,128)} %bitcast.417), kind=kCustom, calls=%fused_computation.5 | custom fusion | flops 1048576 | bytes 12583680 | tf_op jit(solution)/shard_map/scatter-add | solution.py:90
  296.2 14.5 %scatter_fusion.6 = f32[16,8,2,128,128]{4,3,2,1,0:T(8,128)} fusion(f32[16,8,2,128,128]{4,3,2,1,0:T(8,128)} %scatter_fusion.5, s32[64]{0:T(128)S(1)} %reshape.608, f32[64,128,128]{2,1,0:T(8,128)} %bitcast.418), kind=kCustom, calls=%fused_computation.6 | custom fusion | flops 1048576 | bytes 12583680 | tf_op jit(solution)/shard_map/scatter-add | solution.py:90
  310.7 14.5 %scatter_fusion.7 = f32[16,8,2,128,128]{4,3,2,1,0:T(8,128)} fusion(f32[16,8,2,128,128]{4,3,2,1,0:T(8,128)} %scatter_fusion.6, s32[64]{0:T(128)S(1)} %reshape.616, f32[64,128,128]{2,1,0:T(8,128)} %bitcast.419), kind=kCustom, calls=%fused_computation.7 | custom fusion | flops 1048576 | bytes 12583680 | tf_op jit(solution)/shard_map/scatter-add | solution.py:90
  380.2 34.8 %all-reduce.8 = f32[16,1,128]{2,1,0:T(1,128)S(1)} all-reduce(f32[16,1,128]{2,1,0:T(1,128)S(1)} %bitcast.436), channel_id=3, replica_groups=mesh['row'=16,'col_0'=2,'col_1'=4] {'row'}, use_global_device_ids=true, to_apply=%region_18.19.clone | all-reduce | flops 2048 | bytes 16384
  415.7 9.6 %all_to_all.10 = f32[8,1,1,128]{3,2,1,0:T(1,128)S(1)} all-to-all(f32[8,1,1,128]{3,2,1,0:T(1,128)S(1)} %broadcast_in_dim.134), channel_id=1, replica_groups=mesh['row'=16,'col_0'=2,'col_1'=4] {'col_0','col_1'}, dimensions={0} | all-to-all | bytes 8192 | tf_op jit(solution)/shard_map/all_to_all | solution.py:34
  425.2 48.5 %reduce-scatter.2.cloned.1.call-done = f32[1,8,1,2,128,128]{5,4,3,1,2,0:T(8,128)} async-done(((f32[16,8,1,2,128,128]{5,4,3,1,2,0:T(8,128)}), f32[1,8,1,2,128,128]{5,4,3,1,2,0:T(8,128)}) %reduce-scatter.2.cloned.1.call-update) | async-done | bytes 1048592 | tf_op jit(solution)/shard_map/reduce_scatter | solution.py:97
  478.6 25.9 %all-gather = f32[16,1,128]{2,1,0:T(1,128)S(1)} all-gather(f32[1,1,128]{2,1,0:T(1,128)S(1)} %bitcast.449), channel_id=1, replica_groups=mesh['row'=16,'col_0'=2,'col_1'=4] {'row'}, dimensions={0}, use_global_device_ids=true | all-gather | bytes 8704 | tf_op jit(solution)/shard_map/all_gather | solution.py:112
  510.7 8.6 %psum.29 = f32[128]{0:T(128)S(1)} all-reduce(f32[128]{0:T(128)S(1)} %psum.28), channel_id=1, replica_groups=mesh['row'=16,'col_0'=2,'col_1'=4] {'col_1'}, use_global_device_ids=true, to_apply=%region_21.22 | all-reduce | flops 128 | bytes 1024 | tf_op jit(solution)/shard_map/psum | solution.py:44
  519.3 22.3 %all-gather.1 = f32[16,1,128]{2,1,0:T(1,128)S(1)} all-gather(f32[1,1,128]{2,1,0:T(1,128)S(1)} %get-tuple-element.12), channel_id=1, replica_groups=mesh['row'=16,'col_0'=2,'col_1'=4] {'row'}, dimensions={0}, use_global_device_ids=true | all-gather | bytes 8704 | tf_op jit(solution)/shard_map/all_gather | solution.py:112
  546.8 10.1 %psum.31 = f32[128]{0:T(128)S(1)} all-reduce(f32[128]{0:T(128)S(1)} %psum.30), channel_id=1, replica_groups=mesh['row'=16,'col_0'=2,'col_1'=4] {'col_1'}, use_global_device_ids=true, to_apply=%region_23.24 | all-reduce | flops 128 | bytes 1024 | tf_op jit(solution)/shard_map/psum | solution.py:44
  (130 shorter events, 194.5 us)
Async XLA Ops:
  7.2 466.5 %reduce-scatter.2.cloned.1.call-start = ((), (), s32[]{:S(2)}) async-start(), calls=%async_computation.3 | async-start | bytes 17825792 | tf_op jit(solution)/shard_map/reduce_scatter | solution.py:97
  9.3 27.5 %copy-start = (f32[8,512,1024]{2,1,0:T(8,128)S(1)}, f32[8,512,1024]{2,1,0:T(8,128)}, u32[]{:S(2)}) copy-start(f32[8,512,1024]{2,1,0:T(8,128)} %param.9) | copy-start | bytes 50331652
  343.2 5.2 copy-start.5
  343.2 5.2 copy-start.3
  346.5 6.7 %copy-start.10 = (u32[128]{0:T(128)S(1)}, u32[128]{0:T(128)}, u32[]{:S(2)}) copy-start(u32[128]{0:T(128)} %constant.582) | copy-start | bytes 1540
  348.4 9.9 %copy-start.2 = (f32[1024,512]{1,0:T(8,128)S(1)}, f32[1024,512]{1,0:T(8,128)}, u32[]{:S(2)}) copy-start(f32[1024,512]{1,0:T(8,128)} %copy.87) | copy-start | bytes 6291460
  360.8 16.9 %copy-start.1 = (f32[1024,512]{1,0:T(8,128)S(1)}, f32[1024,512]{1,0:T(8,128)}, u32[]{:S(2)}) copy-start(f32[1024,512]{1,0:T(8,128)} %copy.92) | copy-start | bytes 6291460
  369.1 109.5 %copy-start.4 = (f32[128,256]{1,0:T(8,128)S(1)}, f32[128,256]{1,0:T(8,128)}, u32[]{:S(2)}) copy-start(f32[128,256]{1,0:T(8,128)} %param.12) | copy-start | bytes 393220
  369.1 109.6 %copy-start.6 = (f32[128]{0:T(128)S(1)}, f32[128]{0:T(128)}, u32[]{:S(2)}) copy-start(f32[128]{0:T(128)} %param.14) | copy-start | bytes 1540
  373.6 145.7 %copy-start.7 = (f32[128]{0:T(128)S(1)}, f32[128]{0:T(128)}, u32[]{:S(2)}) copy-start(f32[128]{0:T(128)} %param.15) | copy-start | bytes 1540
  373.6 145.7 %copy-start.9 = (f32[128]{0:T(128)S(1)}, f32[128]{0:T(128)}, u32[]{:S(2)}) copy-start(f32[128]{0:T(128)} %param.13) | copy-start | bytes 1540
  473.7 31.0 %all-to-all-start = ((f32[8,1,1,1,2,128,128]{6,5,4,3,2,1,0:T(8,128)}), f32[8,1,1,1,2,128,128]{6,5,4,3,2,1,0:T(8,128)S(1)}, u32[]{:S(2)}, u32[]{:S(2)}) async-start(f32[8,1,1,1,2,128,128]{6,5,4,3,2,1,0:T(8,128)} %bitcast.437), calls=%async_computation.1 | async-start | bytes 2097152 | tf_op jit(solution)/shard_map/all_to_all | solution.py:28
  519.3 38.1 %copy-start.8 = (f32[128]{0:T(128)}, f32[128]{0:T(128)S(1)}, u32[]{:S(2)}) copy-start(f32[128]{0:T(128)S(1)} %get-tuple-element.13) | copy-start | bytes 1540
Sparse Core Ops, SparseCore 0:
  325.3 148.3 reduce-scatter.1
where the time goes:
time: 575 us; the launch traced here: 564 us
  matrix products  148 us (26%)
  other arithmetic  125 us (22%)
  blocking collectives  121 us (21%)
  local copies, waits for them, and re-layouts  102 us (18%)
  waiting for transfers between devices  48.5 us (8%)
  between operations  14.8 us (3%)
    scatter-add x8, other arithmetic, local(): summed_grid.at[row_owner, column_owner, row_place, column_place]  116 us
    dot_general x8, matrix products, local(): lax.dot_general(coupling_week, mapped, (((0,), (0,)), ((), ())), precisio...  71.3 us
    dot_general x8, matrix products, local(): jnp.dot(local_inverse[week_index], coupling_week, precision=highest, pref...  50.9 us
    reduce_scatter x1, waiting for transfers between devices, local(): lax.psum_scatter(summed_grid, 'row', scatter_dimension=0, tiled=True)  48.5 us
    all_gather x2, blocking collectives, local(): whole_iterate = lax.all_gather(solution, 'row', axis=0, tiled=True)  48.3 us
    reshape x8, local copies, waits for them, and re-layouts, local(): contribution.reshape(TOUCHED, BLOCK, TOUCHED, BLOCK).transpose(0, 2, 1, 3)  44.7 us
    unnamed x1, blocking collectives  34.8 us
    psum x4, blocking collectives, over_axes(): return functools.reduce(lax.psum, axes, shard)  28.5 us
  transfers between devices with their start and end apart: 2, of which 1 were waited for; matrix products, arithmetic and copies ran while one was open for 10% of the time, Pallas kernels for 0%

commit v1 on v0

v1 whole, which is shorter than its diff:
```python
import functools

import jax
import jax.numpy as jnp
from jax import lax
from jax.experimental import pallas as pl
from jax.experimental.pallas import tpu as pltpu
from jax.sharding import PartitionSpec as P

BLOCK = 128
BLOCKS = 16
TOUCHED = 8
LOCAL = 512
PASSES = 3
HEAD = 16
COLORS = 3
PIECES = 6
GRID = COLORS * 2 * 64 * PIECES
MESH = pl.DeviceIdType.MESH
f32 = jnp.float32
bf16 = jnp.bfloat16


def split(value):
    high = value.astype(bf16)
    return high, (value - high.astype(f32)).astype(bf16)


def product(left, right):
    total = jnp.dot(left[0], right[0], preferred_element_type=f32)
    if PASSES == 3:
        total += jnp.dot(left[1], right[0], preferred_element_type=f32)
        total += jnp.dot(left[0], right[1], preferred_element_type=f32)
    return total


def piece_base(block):
    core, z = block % 2, (block // 2) % 4
    return core * 384 + (block // 8) * 192 + z * PIECES


def eliminate(
    members, inverse, coupling, rhs, summed, turned_h, turned_l, held_h, held_l, mapped_h, mapped_l
):
    week = pl.program_id(0)

    @pl.when(week == 0)
    def clear():
        @pl.loop(0, GRID // 16)
        def step(index):
            summed[pl.ds(index * 16, 16)] = jnp.zeros((16, 8, BLOCK), f32)

    blocks = [members[week, k] for k in range(TOUCHED)]
    ranks = [
        sum((blocks[j] < blocks[k]).astype(jnp.int32) for j in range(TOUCHED) if j != k)
        for k in range(TOUCHED)
    ]
    place, held = [], []
    for a in range(TOUCHED):
        here = [(ranks[k] == a).astype(jnp.int32) for k in range(TOUCHED)]
        place.append(sum(here[k] * k for k in range(1, TOUCHED)))
        held.append(sum(here[k] * blocks[k] for k in range(TOUCHED)))
    for a in range(TOUCHED):
        columns = coupling[0, :, pl.ds(pl.multiple_of(place[a] * BLOCK, BLOCK), BLOCK)]
        at = slice(a * BLOCK, (a + 1) * BLOCK)
        held_h[:, at], low = split(columns)
        if PASSES == 3:
            held_l[:, at] = low
        at = slice(HEAD + a * BLOCK, HEAD + (a + 1) * BLOCK)
        turned_h[at, :], low = split(columns.T)
        if PASSES == 3:
            turned_l[at, :] = low
    row = lax.broadcasted_iota(jnp.int32, (HEAD, LOCAL), 0)
    first = jnp.where(row == 0, jnp.broadcast_to(rhs[0], (HEAD, LOCAL)), 0.0)
    turned_h[0:HEAD, :], low = split(first)
    if PASSES == 3:
        turned_l[0:HEAD, :] = low
    for n in range(2):
        at = slice(n * 256, n * 256 + 256)
        part = product((turned_h[...], turned_l[...]), split(inverse[0, :, at]))
        mapped_h[:, at], low = split(part)
        if PASSES == 3:
            mapped_l[:, at] = low
    for n in range(4):
        at = slice(n * 256, n * 256 + 256)
        rows = slice(0, HEAD + (n + 1) * 256)
        part = product((mapped_h[rows, :], mapped_l[rows, :]), (held_h[:, at], held_l[:, at]))
        for b in (2 * n, 2 * n + 1):
            lanes = slice((b - 2 * n) * BLOCK, (b - 2 * n + 1) * BLOCK)
            index = 2 * 768 + piece_base(held[b]) + (held[b] // 8) * 96
            index += ((held[b] // 2) % 4) * 24 + PIECES - 1
            summed[index] = summed[index] + part[0:8, lanes]
            for a in range(b + 1):
                low_half = held[a] < 8
                group = jnp.where(low_half, held[a], 15 - held[a])
                piece = jnp.where(low_half, held[b] - held[a], held[b] + 1)
                start = (piece // PIECES) * 768 + piece % PIECES
                tile = part[HEAD + a * BLOCK : HEAD + (a + 1) * BLOCK, lanes].reshape(16, 8, BLOCK)
                places = []
                for s in range(16):
                    base = start + piece_base(group if s < 8 else 15 - group)
                    places.append(base + (s % 8 // 4) * 96 + (s % 4) * 24)
                new = [summed[places[s]] + tile[s] for s in range(16)]
                for s in range(16):
                    summed[places[s]] = new[s]


def device(x, y, z, core):
    return {"row": (x // 2) * 8 + z * 2 + core, "col": (x % 2) * 4 + y}


def combine(
    data, matrix, rhs, prior, weight,
    out_matrix, out_rhs, out_solution,
    own, other, relay1, final1, sum1, relay2, final2, sum2, relay3, final3, sum3,
    land, block_out, blocks_in, partial1, partial2, row1, column1, row2,
    load_sem, pair_send, pair_recv, ring_send, ring_recv,
    tile_send, tile_recv, block_send, block_recv,
    one_send, one_recv, column_send, column_recv, two_send, two_recv,
):
    r, c = lax.axis_index("row"), lax.axis_index("col")
    core, z = r % 2, (r // 2) % 4
    x, y = (r // 8) * 2 + c // 4, c % 4
    me = (x, y, z)

    def neighbour(axis, step):
        at = list(me)
        at[axis] = (me[axis] + step) % 4
        return device(*at, core)

    barrier = pltpu.get_barrier_semaphore()
    partner = {"row": r + 1 - 2 * core, "col": c}
    greeted = [partner] + [neighbour(axis, step) for axis in range(3) for step in (1, 3)]
    for target in greeted:
        pl.semaphore_signal(barrier, inc=1, device_id=target, device_id_type=MESH)

    def cut(ref, lead, position, index, half=None):
        picks = [slice(None)] * position + [index]
        if half is not None:
            size = ref.shape[len(lead)] // 2 if position else ref.shape[len(lead) + 1] // 2
            keep = pl.ds(half * size, size)
            if position:
                picks[0] = keep
            else:
                picks.append(keep)
        return ref.at[(*lead, *picks)]

    steps = (2, 1, 3, 0)

    def loads(color, j):
        at = (me[color] + j) % 4
        src = cut(data, (color, core), color, at)
        return pltpu.make_async_copy(src, cut(own, (color,), color, at), load_sem.at[color, j])

    def pairs(color, j):
        at = (me[color] + j) % 4
        return pltpu.make_async_remote_copy(
            src_ref=cut(data, (color, 1 - core), color, at),
            dst_ref=cut(other, (color,), color, at),
            send_sem=pair_send.at[color, j],
            recv_sem=pair_recv.at[color, j],
            device_id=partner,
            device_id_type=MESH,
        )

    for j in steps:
        for color in range(COLORS):
            loads(color, j).start()
    pl.semaphore_wait(barrier, len(greeted))
    for j in steps:
        for color in range(COLORS):
            pairs(color, j).start()

    def add(target, *terms):
        value = target[...]
        for term in terms:
            value = value + term[...]
        target[...] = value

    def arrived(color, j):
        at = (me[color] + j) % 4
        loads(color, j).wait()
        pairs(color, j).wait_recv()
        add(cut(own, (color,), color, at), cut(other, (color,), color, at))

    axes = ((0, 1, 2), (1, 2, 0), (2, 0, 1))
    spots = ((0, 0), (1, 1), (2, 0))
    waiting = []

    def phase(number, source, relay, final, result, prepare):
        def hop(color, slot, step, src, dst):
            copy = pltpu.make_async_remote_copy(
                src_ref=src,
                dst_ref=dst,
                send_sem=ring_send.at[number, color, slot],
                recv_sem=ring_recv.at[number, color, slot],
                device_id=neighbour(axes[color][number], step),
                device_id_type=MESH,
            )
            return copy

        def source_cut(color, step, half):
            at = (me[axes[color][number]] + step) % 4
            if number == 2:
                return source.at[color, at] if half is None else source.at[color, at, pl.ds(half * 24, 24)]
            return cut(source, (color,), spots[color][number], at, half)

        def landing(ref, color, side, half):
            if half is None:
                return ref.at[color, side]
            size = ref.shape[2] // 2
            return ref.at[color, side, pl.ds(half * size, size)]

        def away(color, side):
            return hop(color, side, (1, 3)[side], source_cut(color, 2, side), relay.at[color, side])

        def near(color, side, half):
            step = (1, 3)[side]
            return hop(
                color, 2 + 2 * side + half, step,
                source_cut(color, step, half), landing(final, color, side, half),
            )

        for color in range(COLORS):
            prepare(color, 2)
            for side in range(2):
                away(color, side).start()
        for color in range(COLORS):
            for side in range(2):
                prepare(color, (1, 3)[side])
                near(color, side, 1 - side).start()
        for color in range(COLORS):
            for side in range(2):
                away(color, side).wait_recv()
                add(source_cut(color, (1, 3)[side], side), relay.at[color, side])
                near(color, side, side).start()
        for color in range(COLORS):
            prepare(color, 0)
            for side in range(2):
                for half in range(2):
                    near(color, side, half).wait_recv()
            mine = source_cut(color, 0, None)
            result[color] = mine[...] + final[color, 0] + final[color, 1]
        for color in range(COLORS):
            for side in range(2):
                waiting.append(away(color, side))
                for half in range(2):
                    waiting.append(near(color, side, half))

    def nothing(color, j):
        pass

    phase(0, own, relay1, final1, sum1, arrived)
    phase(1, sum1, relay2, final2, sum2, nothing)
    phase(2, sum2, relay3, final3, sum3, nothing)

    low_half = r < 8
    group = jnp.where(low_half, r, 15 - r)
    strip = jnp.where(low_half, c, c + 8)

    def piece(t):
        return sum3.at[t // PIECES, pl.ds((t % PIECES) * 8, 8)]

    def tile_copy(t, mirrored):
        first = t < 16 - group
        i = jnp.where(first, group, 15 - group)
        j = jnp.where(first, group + t, t - 1)
        row, column = (j, i) if mirrored else (i, j)
        copy = pltpu.make_async_remote_copy(
            src_ref=piece(t),
            dst_ref=land.at[column % 2, strip],
            send_sem=tile_send.at[t, int(mirrored)],
            recv_sem=tile_recv.at[column % 2, strip],
            device_id={"row": row, "col": column // 2},
            device_id_type=MESH,
        )
        mine = (row == r) & (column // 2 == c)
        wanted = (i != j) if mirrored else None
        return copy, mine, wanted, column % 2

    holder = c == r // 2

    def to_column(d):
        return pltpu.make_async_remote_copy(
            src_ref=block_out,
            dst_ref=blocks_in.at[1 + r % 2],
            send_sem=block_send.at[d],
            recv_sem=block_recv.at[1 + r % 2],
            device_id={"row": (r + d) % 16, "col": c},
            device_id_type=MESH,
        )

    def to_row(d):
        return pltpu.make_async_remote_copy(
            src_ref=block_out,
            dst_ref=blocks_in.at[0],
            send_sem=block_send.at[15 + d],
            recv_sem=block_recv.at[0],
            device_id={"row": r, "col": (c + d) % 8},
            device_id_type=MESH,
        )

    @pl.when(holder)
    def hand_out():
        reduced = rhs[...] - sum3[2, 40:41, :]
        row = lax.broadcasted_iota(jnp.int32, (8, BLOCK), 0)
        value = jnp.where(row == 0, reduced, jnp.where(row == 1, prior[...], weight[...]))
        block_out[...] = value
        blocks_in[0] = value
        blocks_in[1 + r % 2] = value
        for d in range(1, 16):
            to_column(d).start()
        for d in range(1, 8):
            to_row(d).start()

    for t in range(17):
        for mirrored in (False, True):
            copy, mine, wanted, side = tile_copy(t, mirrored)
            away = jnp.logical_not(mine)
            if wanted is not None:
                mine, away = mine & wanted, away & wanted

            @pl.when(away)
            def send():
                copy.start()

            @pl.when(mine)
            def keep():
                land[side, strip] = piece(t)[...]

    def receive(buffer, semaphore):
        pltpu.make_async_remote_copy(
            src_ref=buffer,
            dst_ref=buffer,
            send_sem=semaphore,
            recv_sem=semaphore,
            device_id=partner,
            device_id_type=MESH,
        ).wait_recv()

    for side in range(2):
        column = 2 * c + side
        low = jnp.minimum(r, column)
        owner = jnp.where(low < 8, low, 15 - low)
        for s in range(16):
            row = owner if s < 8 else 15 - owner

            @pl.when(jnp.logical_not((row == r) & (c == s % 8)))
            def wait():
                receive(land.at[side, s], tile_recv.at[side, s])

    tiles = []
    for side in range(2):
        found = land[side].reshape(BLOCK, BLOCK)
        found = jnp.where(r > 2 * c + side, found.T, found)
        lanes = slice(side * BLOCK, (side + 1) * BLOCK)
        tile = matrix[:, lanes] - found
        out_matrix[:, lanes] = tile
        tiles.append(tile)

    @pl.when(jnp.logical_not(holder))
    def row_block():
        receive(blocks_in.at[0], block_recv.at[0])

    for side in range(2):

        @pl.when(r != 2 * c + side)
        def column_block():
            receive(blocks_in.at[1 + side], block_recv.at[1 + side])

    reduced = blocks_in[0, 0:1, :]
    out_rhs[...] = reduced

    def matvec(first, second):
        spread = tiles[0] * first + tiles[1] * second
        return jnp.broadcast_to(jnp.sum(spread.T, axis=0, keepdims=True), (8, BLOCK))

    def along_row(d, source, target, sends, recvs):
        return pltpu.make_async_remote_copy(
            src_ref=source,
            dst_ref=target.at[c],
            send_sem=sends.at[d],
            recv_sem=recvs.at[c],
            device_id={"row": r, "col": (c + d) % 8},
            device_id_type=MESH,
        )

    def along_column(d):
        return pltpu.make_async_remote_copy(
            src_ref=partial1,
            dst_ref=column1.at[r % 2, c],
            send_sem=column_send.at[d],
            recv_sem=column_recv.at[r % 2, c],
            device_id={"row": (r + d) % 16, "col": r // 2},
            device_id_type=MESH,
        )

    value = matvec(blocks_in[1, 1:2, :], blocks_in[2, 1:2, :])
    partial1[...] = value
    row1[c] = value
    for d in range(1, 16):
        along_column(d).start()

    @pl.when(jnp.logical_not(holder))
    def last_column():
        along_column(0).start()

    @pl.when(holder)
    def own_column():
        column1[r % 2, c] = value

    for d in range(1, 8):
        along_row(d, partial1, row1, one_send, one_recv).start()

    def gather_row(target, recvs):
        for s in range(8):

            @pl.when(c != s)
            def wait():
                receive(target.at[s], recvs.at[s])

    def total(ref):
        value = ref[0, 0:1, :]
        for s in range(1, 8):
            value = value + ref[s, 0:1, :]
        return value

    def updated(block, product):
        return block[1:2, :] + block[2:3, :] * (block[0:1, :] - product)

    for side in range(2):
        for s in range(8):

            @pl.when(jnp.logical_not((r == 2 * c + side) & (c == s)))
            def wait():
                receive(column1.at[side, s], column_recv.at[side, s])

    first = [updated(blocks_in[1 + side], total(column1.at[side])) for side in range(2)]
    value = matvec(*first)
    partial2[...] = value
    row2[c] = value
    for d in range(1, 8):
        along_row(d, partial2, row2, two_send, two_recv).start()
    gather_row(row1, one_recv)
    mine = updated(blocks_in[0], total(row1))
    gather_row(row2, two_recv)
    out_solution[...] = mine + weight[...] * (reduced - total(row2))

    for color in range(COLORS):
        for j in steps:
            pairs(color, j).wait_send()
    for copy in waiting:
        copy.wait_send()
    for t in range(17):
        for mirrored in (False, True):
            copy, mine, wanted, side = tile_copy(t, mirrored)
            away = jnp.logical_not(mine)
            if wanted is not None:
                away = away & wanted

            @pl.when(away)
            def sent():
                copy.wait_send()

    @pl.when(holder)
    def handed():
        for d in range(1, 16):
            to_column(d).wait_send()
        for d in range(1, 8):
            to_row(d).wait_send()

    for d in range(1, 16):
        along_column(d).wait_send()

    @pl.when(jnp.logical_not(holder))
    def last_sent():
        along_column(0).wait_send()

    for d in range(1, 8):
        along_row(d, partial1, row1, one_send, one_recv).wait_send()
        along_row(d, partial2, row2, two_send, two_recv).wait_send()


def partial_sum(local_inverse, coupling, local_rhs, members):
    weeks = local_inverse.shape[0]
    mapped = pltpu.VMEM((HEAD + TOUCHED * BLOCK, LOCAL), bf16)
    held = pltpu.VMEM((LOCAL, TOUCHED * BLOCK), bf16)
    return pl.pallas_call(
        eliminate,
        grid_spec=pltpu.PrefetchScalarGridSpec(
            num_scalar_prefetch=1,
            grid=(weeks,),
            in_specs=[
                pl.BlockSpec((1, LOCAL, LOCAL), lambda w, m: (w, 0, 0)),
                pl.BlockSpec((1, LOCAL, TOUCHED * BLOCK), lambda w, m: (w, 0, 0)),
                pl.BlockSpec((1, 1, LOCAL), lambda w, m: (w, 0, 0)),
            ],
            out_specs=pl.BlockSpec((GRID, 8, BLOCK), lambda w, m: (0, 0, 0)),
            scratch_shapes=[mapped, mapped, held, held, mapped, mapped],
        ),
        out_shape=jax.ShapeDtypeStruct((GRID, 8, BLOCK), f32),
        compiler_params=pltpu.CompilerParams(
            dimension_semantics=("arbitrary",), vmem_limit_bytes=60 * 2**20
        ),
        name="eliminate",
    )(members, local_inverse, coupling, local_rhs.reshape(weeks, 1, LOCAL))


def combined(summed, shared_matrix, shared_rhs, prior_solution, preconditioner):
    rows, columns = shared_matrix.shape
    vmem = pl.BlockSpec(memory_space=pltpu.VMEM)
    strip = PIECES * 8
    dma = pltpu.SemaphoreType.DMA

    def buffer(*shape):
        return pltpu.VMEM(shape, f32)

    return pl.pallas_call(
        combine,
        in_specs=[pl.BlockSpec(memory_space=pl.ANY)] + [vmem] * 4,
        out_specs=[vmem] * 3,
        out_shape=[
            jax.ShapeDtypeStruct((rows, columns), f32),
            jax.ShapeDtypeStruct((1, rows), f32),
            jax.ShapeDtypeStruct((1, rows), f32),
        ],
        scratch_shapes=[
            buffer(COLORS, 4, 4, 4, strip, BLOCK),
            buffer(COLORS, 4, 4, 4, strip, BLOCK),
            buffer(COLORS, 2, 2, 4, strip, BLOCK),
            buffer(COLORS, 2, 4, 4, strip, BLOCK),
            buffer(COLORS, 4, 4, strip, BLOCK),
            buffer(COLORS, 2, 2, strip, BLOCK),
            buffer(COLORS, 2, 4, strip, BLOCK),
            buffer(COLORS, 4, strip, BLOCK),
            buffer(COLORS, 2, strip // 2, BLOCK),
            buffer(COLORS, 2, strip, BLOCK),
            buffer(COLORS, strip, BLOCK),
            buffer(2, 16, 8, BLOCK),
            buffer(8, BLOCK),
            buffer(3, 8, BLOCK),
            buffer(8, BLOCK),
            buffer(8, BLOCK),
            buffer(8, 8, BLOCK),
            buffer(2, 8, 8, BLOCK),
            buffer(8, 8, BLOCK),
            dma((COLORS, 4)),
            dma((COLORS, 4)),
            dma((COLORS, 4)),
            dma((3, COLORS, 6)),
            dma((3, COLORS, 6)),
            dma((17, 2)),
            dma((2, 16)),
            dma((23,)),
            dma((3,)),
            dma((8,)),
            dma((8,)),
            dma((16,)),
            dma((2, 8)),
            dma((8,)),
            dma((8,)),
        ],
        compiler_params=pltpu.CompilerParams(
            collective_id=0, has_side_effects=True, vmem_limit_bytes=40 * 2**20
        ),
        name="combine",
    )(
        summed.reshape(COLORS, 2, 4, 4, 4, strip, BLOCK),
        shared_matrix,
        shared_rhs.reshape(1, rows),
        prior_solution.reshape(1, rows),
        preconditioner.reshape(1, rows),
    )


def local(
    local_inverse,
    coupling,
    local_rhs,
    members,
    shared_matrix,
    shared_rhs,
    prior_solution,
    preconditioner,
):
    summed = partial_sum(local_inverse, coupling, local_rhs, members)
    reduced_matrix, reduced_rhs, solution = combined(
        summed, shared_matrix, shared_rhs, prior_solution, preconditioner
    )
    return reduced_matrix, reduced_rhs.reshape(-1), solution.reshape(-1)


def solution(mesh):
    both = ("row", "col")
    placed = (
        P(both, None, None),
        P(both, None, None),
        P(both, None),
        P(both, None),
        P("row", "col"),
        P("row"),
        P("row"),
        P("row"),
    )
    return jax.shard_map(
        local,
        mesh=mesh,
        in_specs=placed,
        out_specs=(P("row", "col"), P("row"), P("row")),
        check_vma=False,
    )
```

time: 575 us -> 114 us (0.20); the launches traced: 564 us -> 112 us
  matrix products: 148 us -> 0 us
  other arithmetic: 125 us -> 0 us
  blocking collectives: 121 us -> 0 us
  Pallas kernels: 0 us -> 105 us
  local copies, waits for them, and re-layouts: 102 us -> 6.7 us
  waiting for transfers between devices: 48.5 us -> 0 us
  between operations: 14.8 us -> 0.67 us
    dot_general x26 -> x0, matrix products: 148 us -> none  [the longest x8 71.3 us: local(): lax.dot_general(coupling_week, mapped, (((0,), (0,)), ((), ())), precisio...]
    scatter-add x16 -> x0, other arithmetic: 122 us -> none  [the longest x8 116 us: local(): summed_grid.at[row_owner, column_owner, row_place, column_place]]
    pallas_call x0 -> x2, Pallas kernels: none -> 105 us  [the longest x1 57 us: combined(): pl.pallas_call(combine, in_specs=[pl.BlockSpec(memory_space=pl.ANY)] + [v...]
    reduce_scatter x1 -> x0, waiting for transfers between devices: 48.5 us -> none  [local(): lax.psum_scatter(summed_grid, 'row', scatter_dimension=0, tiled=True)]
    all_gather x2 -> x0, blocking collectives: 48.3 us -> none  [local(): whole_iterate = lax.all_gather(solution, 'row', axis=0, tiled=True)]
    reshape x8 -> x1, local copies, waits for them, and re-layouts: 44.7 us -> 1.33 us  [partial_sum(): local_rhs.reshape(weeks, 1, LOCAL)]
    unnamed x1 -> x0, blocking collectives: 34.8 us -> none
    psum x4 -> x0, blocking collectives: 28.5 us -> none  [over_axes(): return functools.reduce(lax.psum, axes, shard)]
  transfers between devices with their start and end apart: 2 -> 0, of which waited for: 1 -> 0; matrix products, arithmetic and copies ran while one was open for 10% -> 0% of each run, Pallas kernels for 0% -> 0%
where the time goes in v1:
time: 114 us; the launch traced here: 112 us
  Pallas kernels  105 us (92%)
  local copies, waits for them, and re-layouts  6.7 us (6%)
    pallas_call x1, Pallas kernels, combined(): pl.pallas_call(combine, in_specs=[pl.BlockSpec(memory_space=pl.ANY)] + [v...  57 us
    pallas_call x1, Pallas kernels, partial_sum(): pl.pallas_call(eliminate, grid_spec=pltpu.PrefetchScalarGridSpec(num_scal...  47.8 us
    unnamed x13, local copies, waits for them, and re-layouts  5.37 us

profile of v1, /device:TPU:40, one launch (start us, length us, event | category | flops | bytes accessed | tf_op | source)
XLA Modules:
  0.0 112.2 jit_solution(13133721946390880205)
XLA Ops:
  0.6 1.3 %reshape.27.rhs = f32[8,1,512]{2,1,0:T(1,128)} reshape(f32[8,512]{1,0:T(8,128)} %param.10) | data formatting | bytes 32768 | tf_op jit(solution)/shard_map/reshape | solution.py:506
  2.0 0.0 copy-start.1
  2.0 0.0 copy-start.2
  2.0 0.0 copy-start.3
  2.0 0.0 copy-start.4
  2.0 47.8 %eliminate.1 = f32[2304,8,128]{2,1,0:T(8,128)} custom-call(s32[8,8]{1,0:T(8,128)} %members.1, f32[8,512,512]{2,1,0:T(8,128)} %inverse.1, f32[8,512,1024]{2,1,0:T(8,128)} %coupling.1, f32[8,1,512]{2,1,0:T(1,128)} %reshape.27.rhs), custom_call_target="tpu_custom_call" | custom-call | tf_op jit(solution)/shard_map/eliminate/pallas_call | solution.py:488
  49.8 0.0 copy-done.1
  49.8 0.0 copy-done.2
  49.8 0.0 copy-done.3
  49.8 0.0 copy-done.4
  49.8 0.0 copy-start
  49.9 3.7 %copy-done = f32[2304,8,128]{2,1,0:T(8,128)S(1)} copy-done((f32[2304,8,128]{2,1,0:T(8,128)S(1)}, f32[2304,8,128]{2,1,0:T(8,128)}, u32[]{:S(2)}) %copy-start) | copy-done | bytes 9437208
  53.5 57.0 %combine.1 = (f32[128,256]{1,0:T(8,128)S(1)}, f32[1,128]{1,0:T(1,128)S(1)}, f32[1,128]{1,0:T(1,128)S(1)}) custom-call(f32[3,2,4,4,4,48,128]{6,5,4,3,2,1,0:T(8,128)S(1)} %bitcast.6, f32[128,256]{1,0:T(8,128)S(1)} %copy-done.1, f32[1,128]{1,0:T(1,128)S(1)} %bitcast.7, f32[1,128]{1,0:T(1,128)S(1)} %bitcast.8, f32[1,128]{1,0:T(1,128)S(1)} %bitcast.9), custom_call_target="tpu_custom_call" | custom-call | tf_op jit(solution)/shard_map/combine/pallas_call | solution.py:518
  110.5 0.7 copy.14
  111.2 0.5 copy.15
  111.7 0.5 copy.16
Async XLA Ops:
  2.0 47.9 %copy-start.1 = (f32[128,256]{1,0:T(8,128)S(1)}, f32[128,256]{1,0:T(8,128)}, u32[]{:S(2)}) copy-start(f32[128,256]{1,0:T(8,128)} %matrix.1) | copy-start | bytes 393220
  2.0 47.9 %copy-start.2 = (f32[128]{0:T(128)S(1)}, f32[128]{0:T(128)}, u32[]{:S(2)}) copy-start(f32[128]{0:T(128)} %param.13) | copy-start | bytes 1540
  2.0 47.9 %copy-start.3 = (f32[128]{0:T(128)S(1)}, f32[128]{0:T(128)}, u32[]{:S(2)}) copy-start(f32[128]{0:T(128)} %param.14) | copy-start | bytes 1540
  2.0 47.9 %copy-start.4 = (f32[128]{0:T(128)S(1)}, f32[128]{0:T(128)}, u32[]{:S(2)}) copy-start(f32[128]{0:T(128)} %param.15) | copy-start | bytes 1540
  49.8 3.7 %copy-start = (f32[2304,8,128]{2,1,0:T(8,128)S(1)}, f32[2304,8,128]{2,1,0:T(8,128)}, u32[]{:S(2)}) copy-start(f32[2304,8,128]{2,1,0:T(8,128)} %eliminate.1) | copy-start | bytes 28311556

commit v2 on v1

--- a/solution.py
+++ b/solution.py
@@ -40,69 +40,153 @@
 
 
 def eliminate(
-    members, inverse, coupling, rhs, summed, turned_h, turned_l, held_h, held_l, mapped_h, mapped_l
+    members, inverse, coupling, rhs, summed,
+    inverse_in, coupling_in, in_sem,
+    turned, held, kept, mapped,
 ):
-    week = pl.program_id(0)
-
-    @pl.when(week == 0)
-    def clear():
-        @pl.loop(0, GRID // 16)
-        def step(index):
-            summed[pl.ds(index * 16, 16)] = jnp.zeros((16, 8, BLOCK), f32)
-
-    blocks = [members[week, k] for k in range(TOUCHED)]
-    ranks = [
-        sum((blocks[j] < blocks[k]).astype(jnp.int32) for j in range(TOUCHED) if j != k)
-        for k in range(TOUCHED)
-    ]
-    place, held = [], []
-    for a in range(TOUCHED):
-        here = [(ranks[k] == a).astype(jnp.int32) for k in range(TOUCHED)]
-        place.append(sum(here[k] * k for k in range(1, TOUCHED)))
-        held.append(sum(here[k] * blocks[k] for k in range(TOUCHED)))
-    for a in range(TOUCHED):
-        columns = coupling[0, :, pl.ds(pl.multiple_of(place[a] * BLOCK, BLOCK), BLOCK)]
-        at = slice(a * BLOCK, (a + 1) * BLOCK)
-        held_h[:, at], low = split(columns)
-        if PASSES == 3:
-            held_l[:, at] = low
-        at = slice(HEAD + a * BLOCK, HEAD + (a + 1) * BLOCK)
-        turned_h[at, :], low = split(columns.T)
-        if PASSES == 3:
-            turned_l[at, :] = low
-    row = lax.broadcasted_iota(jnp.int32, (HEAD, LOCAL), 0)
-    first = jnp.where(row == 0, jnp.broadcast_to(rhs[0], (HEAD, LOCAL)), 0.0)
-    turned_h[0:HEAD, :], low = split(first)
-    if PASSES == 3:
-        turned_l[0:HEAD, :] = low
-    for n in range(2):
-        at = slice(n * 256, n * 256 + 256)
-        part = product((turned_h[...], turned_l[...]), split(inverse[0, :, at]))
-        mapped_h[:, at], low = split(part)
-        if PASSES == 3:
-            mapped_l[:, at] = low
-    for n in range(4):
-        at = slice(n * 256, n * 256 + 256)
-        rows = slice(0, HEAD + (n + 1) * 256)
-        part = product((mapped_h[rows, :], mapped_l[rows, :]), (held_h[:, at], held_l[:, at]))
-        for b in (2 * n, 2 * n + 1):
-            lanes = slice((b - 2 * n) * BLOCK, (b - 2 * n + 1) * BLOCK)
-            index = 2 * 768 + piece_base(held[b]) + (held[b] // 8) * 96
-            index += ((held[b] // 2) % 4) * 24 + PIECES - 1
-            summed[index] = summed[index] + part[0:8, lanes]
-            for a in range(b + 1):
-                low_half = held[a] < 8
-                group = jnp.where(low_half, held[a], 15 - held[a])
-                piece = jnp.where(low_half, held[b] - held[a], held[b] + 1)
-                start = (piece // PIECES) * 768 + piece % PIECES
-                tile = part[HEAD + a * BLOCK : HEAD + (a + 1) * BLOCK, lanes].reshape(16, 8, BLOCK)
-                places = []
-                for s in range(16):
-                    base = start + piece_base(group if s < 8 else 15 - group)
-                    places.append(base + (s % 8 // 4) * 96 + (s % 4) * 24)
-                new = [summed[places[s]] + tile[s] for s in range(16)]
-                for s in range(16):
-                    summed[places[s]] = new[s]
+    weeks = inverse.shape[0]
+
+    def fetch(week, slot):
+        return (
+            pltpu.make_async_copy(inverse.at[week], inverse_in[slot], in_sem.at[slot, 0]),
+            pltpu.make_async_copy(coupling.at[week], coupling_in[slot], in_sem.at[slot, 1]),
+        )
+
+    def start(week, slot):
+        for copy in fetch(week, slot):
+            copy.start()
+
+    def wait(week, slot):
+        for copy in fetch(week, slot):
+            copy.wait()
+
+    def order(week):
+        blocks = [members[week, k] for k in range(TOUCHED)]
+        ranks = [
+            sum((blocks[j] < blocks[k]).astype(jnp.int32) for j in range(TOUCHED) if j != k)
+            for k in range(TOUCHED)
+        ]
+        place, sorted_blocks = [], []
+        for a in range(TOUCHED):
+            here = [(ranks[k] == a).astype(jnp.int32) for k in range(TOUCHED)]
+            place.append(sum(here[k] * k for k in range(1, TOUCHED)))
+            sorted_blocks.append(sum(here[k] * blocks[k] for k in range(TOUCHED)))
+        return place, sorted_blocks
+
+    def prepare(week, slot):
+        place, _ = order(week)
+
+        def columns_of(a):
+            def work():
+                columns = coupling_in[slot][:, pl.ds(pl.multiple_of(place[a] * BLOCK, BLOCK), BLOCK)]
+                at = slice(a * BLOCK, (a + 1) * BLOCK)
+                held[slot][0][:, at], held[slot][1][:, at] = split(columns)
+                at = slice(HEAD + a * BLOCK, HEAD + (a + 1) * BLOCK)
+                turned[slot][0][at, :], turned[slot][1][at, :] = split(columns.T)
+
+            return work
+
+        def inverse_part(n):
+            def work():
+                at = slice(n * 128, n * 128 + 128)
+                kept[slot][0][at, :], kept[slot][1][at, :] = split(inverse_in[slot][at, :])
+
+            return work
+
+        def head():
+            row = lax.broadcasted_iota(jnp.int32, (HEAD, LOCAL), 0)
+            first = jnp.where(row == 0, jnp.broadcast_to(rhs[pl.ds(week, 1), :], (HEAD, LOCAL)), 0.0)
+            turned[slot][0][0:HEAD, :], turned[slot][1][0:HEAD, :] = split(first)
+
+        return [head] + [inverse_part(n) for n in range(4)] + [columns_of(a) for a in range(TOUCHED)]
+
+    def multiply(week, slot):
+        _, blocks = order(week)
+
+        def map_part(n, rows):
+            def work():
+                at = slice(n * 256, n * 256 + 256)
+                part = product(
+                    (turned[slot][0][rows, :], turned[slot][1][rows, :]),
+                    (kept[slot][0][:, at], kept[slot][1][:, at]),
+                )
+                mapped[0][rows, at], mapped[1][rows, at] = split(part)
+
+            return work
+
+        def add_tiles(n, part, offset, places):
+            for b in (2 * n, 2 * n + 1):
+                lanes = slice((b - 2 * n) * BLOCK, (b - 2 * n + 1) * BLOCK)
+                for a in places:
+                    if a == -1:
+                        index = 2 * 768 + piece_base(blocks[b]) + (blocks[b] // 8) * 96
+                        index += ((blocks[b] // 2) % 4) * 24 + PIECES - 1
+                        summed[index] = summed[index] + part[0:8, lanes]
+                    elif a <= b:
+                        low_half = blocks[a] < 8
+                        group = jnp.where(low_half, blocks[a], 15 - blocks[a])
+                        piece = jnp.where(low_half, blocks[b] - blocks[a], blocks[b] + 1)
+                        first = (piece // PIECES) * 768 + piece % PIECES
+                        top = HEAD + a * BLOCK - offset
+                        tile = part[top : top + BLOCK, lanes].reshape(16, 8, BLOCK)
+                        spots = []
+                        for s in range(16):
+                            base = first + piece_base(group if s < 8 else 15 - group)
+                            spots.append(base + (s % 8 // 4) * 96 + (s % 4) * 24)
+                        new = [summed[spots[s]] + tile[s] for s in range(16)]
+                        for s in range(16):
+                            summed[spots[s]] = new[s]
+
+        def pair_part(n, m):
+            def work():
+                low = 0 if m == 0 else HEAD + m * 256
+                rows = slice(low, HEAD + (m + 1) * 256)
+                at = slice(n * 256, n * 256 + 256)
+                part = product(
+                    (mapped[0][rows, :], mapped[1][rows, :]),
+                    (held[slot][0][:, at], held[slot][1][:, at]),
+                )
+                add_tiles(n, part, low, ([-1] if m == 0 else []) + [2 * m, 2 * m + 1])
+
+            return work
+
+        cuts = [slice(0, HEAD + 256)] + [slice(HEAD + k * 256, HEAD + k * 256 + 256) for k in (1, 2, 3)]
+        first = [map_part(n, rows) for rows in cuts for n in range(2)]
+        return first + [pair_part(n, m) for n in range(4) for m in range(n + 1)]
+
+    def half_step(week, slot):
+        other = 1 - slot
+
+        @pl.when(week + 1 < weeks)
+        def arrive():
+            wait(week + 1, other)
+
+        @pl.when(week + 2 < weeks)
+        def ahead():
+            start(week + 2, slot)
+
+        work = multiply(week, slot)
+        more = prepare(jnp.minimum(week + 1, weeks - 1), other)
+        for index, item in enumerate(work):
+            item()
+            if index < len(more):
+                more[index]()
+
+    start(0, 0)
+    start(1, 1)
+
+    @pl.loop(0, GRID // 16)
+    def clear(index):
+        summed[pl.ds(index * 16, 16)] = jnp.zeros((16, 8, BLOCK), f32)
+
+    wait(0, 0)
+    for item in prepare(0, 0):
+        item()
+
+    @pl.loop(0, weeks // 2)
+    def step(index):
+        half_step(2 * index, 0)
+        half_step(2 * index + 1, 1)
 
 
 def device(x, y, z, core):
@@ -112,7 +196,7 @@
 def combine(
     data, matrix, rhs, prior, weight,
     out_matrix, out_rhs, out_solution,
-    own, other, relay1, final1, sum1, relay2, final2, sum2, relay3, final3, sum3,
+    own, other, relay1, final1, sum1, relay2, final2, sum2, final3, sum3,
     land, block_out, blocks_in, partial1, partial2, row1, column1, row2,
     load_sem, pair_send, pair_recv, ring_send, ring_recv,
     tile_send, tile_recv, block_send, block_recv,
@@ -134,42 +218,40 @@
     for target in greeted:
         pl.semaphore_signal(barrier, inc=1, device_id=target, device_id_type=MESH)
 
-    def cut(ref, lead, position, index, half=None):
-        picks = [slice(None)] * position + [index]
+    strip_rows = [pl.ds(24 * part, 24) for part in range(2)]
+
+    def cut(ref, lead, dims, position, index, part, half=None):
+        picks = [slice(None)] * dims
+        picks[position] = index
         if half is not None:
-            size = ref.shape[len(lead)] // 2 if position else ref.shape[len(lead) + 1] // 2
-            keep = pl.ds(half * size, size)
-            if position:
-                picks[0] = keep
-            else:
-                picks.append(keep)
-        return ref.at[(*lead, *picks)]
-
-    steps = (2, 1, 3, 0)
-
-    def loads(color, j):
+            picks[0 if position else 1] = pl.ds(2 * half, 2)
+        return ref.at[(*lead, *picks, strip_rows[part])]
+
+    def loads(color, j, part):
         at = (me[color] + j) % 4
-        src = cut(data, (color, core), color, at)
-        return pltpu.make_async_copy(src, cut(own, (color,), color, at), load_sem.at[color, j])
-
-    def pairs(color, j):
+        src = cut(data, (color, core), 3, color, at, part)
+        dst = cut(own, (color,), 3, color, at, part)
+        return pltpu.make_async_copy(src, dst, load_sem.at[part, color, j])
+
+    def pairs(color, j, part):
         at = (me[color] + j) % 4
         return pltpu.make_async_remote_copy(
-            src_ref=cut(data, (color, 1 - core), color, at),
-            dst_ref=cut(other, (color,), color, at),
-            send_sem=pair_send.at[color, j],
-            recv_sem=pair_recv.at[color, j],
+            src_ref=cut(data, (color, 1 - core), 3, color, at, part),
+            dst_ref=cut(other, (color,), 3, color, at, part),
+            send_sem=pair_send.at[part, color, j],
+            recv_sem=pair_recv.at[part, color, j],
             device_id=partner,
             device_id_type=MESH,
         )
 
-    for j in steps:
+    everything = [(2, 0), (1, 0), (3, 0), (2, 1), (0, 0), (1, 1), (3, 1), (0, 1)]
+    for j, part in everything:
         for color in range(COLORS):
-            loads(color, j).start()
+            loads(color, j, part).start()
     pl.semaphore_wait(barrier, len(greeted))
-    for j in steps:
+    for j, part in everything:
         for color in range(COLORS):
-            pairs(color, j).start()
+            pairs(color, j, part).start()
 
     def add(target, *terms):
         value = target[...]
@@ -177,82 +259,113 @@
             value = value + term[...]
         target[...] = value
 
-    def arrived(color, j):
+    def arrived(color, j, part):
         at = (me[color] + j) % 4
-        loads(color, j).wait()
-        pairs(color, j).wait_recv()
-        add(cut(own, (color,), color, at), cut(other, (color,), color, at))
+        loads(color, j, part).wait()
+        pairs(color, j, part).wait_recv()
+        add(cut(own, (color,), 3, color, at, part), cut(other, (color,), 3, color, at, part))
 
     axes = ((0, 1, 2), (1, 2, 0), (2, 0, 1))
     spots = ((0, 0), (1, 1), (2, 0))
     waiting = []
 
-    def phase(number, source, relay, final, result, prepare):
-        def hop(color, slot, step, src, dst):
-            copy = pltpu.make_async_remote_copy(
-                src_ref=src,
-                dst_ref=dst,
-                send_sem=ring_send.at[number, color, slot],
-                recv_sem=ring_recv.at[number, color, slot],
-                device_id=neighbour(axes[color][number], step),
-                device_id_type=MESH,
-            )
-            return copy
-
-        def source_cut(color, step, half):
+    def hop(number, color, slot, step, part, src, dst):
+        return pltpu.make_async_remote_copy(
+            src_ref=src,
+            dst_ref=dst,
+            send_sem=ring_send.at[part, number, color, slot],
+            recv_sem=ring_recv.at[part, number, color, slot],
+            device_id=neighbour(axes[color][number], step),
+            device_id_type=MESH,
+        )
+
+    def ring(number, source, relay, final, result, prepare):
+        dims = 3 - number
+
+        def source_cut(color, step, part, half=None):
             at = (me[axes[color][number]] + step) % 4
-            if number == 2:
-                return source.at[color, at] if half is None else source.at[color, at, pl.ds(half * 24, 24)]
-            return cut(source, (color,), spots[color][number], at, half)
-
-        def landing(ref, color, side, half):
-            if half is None:
-                return ref.at[color, side]
-            size = ref.shape[2] // 2
-            return ref.at[color, side, pl.ds(half * size, size)]
-
-        def away(color, side):
-            return hop(color, side, (1, 3)[side], source_cut(color, 2, side), relay.at[color, side])
-
-        def near(color, side, half):
+            return cut(source, (color,), dims, spots[color][number], at, part, half)
+
+        def landing(color, side, part, half=None):
+            picks = [slice(None)] * (dims - 1)
+            if half is not None:
+                picks[0] = pl.ds(2 * half, 2)
+            return final.at[(color, side, *picks, strip_rows[part])]
+
+        def relayed(color, side, part):
+            return relay.at[(color, side, *[slice(None)] * (dims - 1), strip_rows[part])]
+
+        def away(color, side, part):
+            src = source_cut(color, 2, part, side)
+            return hop(number, color, side, (1, 3)[side], part, src, relayed(color, side, part))
+
+        def near(color, side, part, half):
             step = (1, 3)[side]
-            return hop(
-                color, 2 + 2 * side + half, step,
-                source_cut(color, step, half), landing(final, color, side, half),
-            )
-
+            src = source_cut(color, step, part, half)
+            dst = landing(color, side, part, half)
+            return hop(number, color, 2 + 2 * side + half, step, part, src, dst)
+
+        def far(part):
+            for color in range(COLORS):
+                prepare(color, 2, part)
+                for side in range(2):
+                    away(color, side, part).start()
+                    waiting.append(away(color, side, part))
+
+        def close(part):
+            for color in range(COLORS):
+                for side in range(2):
+                    prepare(color, (1, 3)[side], part)
+                    near(color, side, part, 1 - side).start()
+
+        def pass_on(part):
+            for color in range(COLORS):
+                for side in range(2):
+                    away(color, side, part).wait_recv()
+                    add(source_cut(color, (1, 3)[side], part, side), relayed(color, side, part))
+                    near(color, side, part, side).start()
+
+        def finish(part):
+            for color in range(COLORS):
+                prepare(color, 0, part)
+                for side in range(2):
+                    for half in range(2):
+                        near(color, side, part, half).wait_recv()
+                        waiting.append(near(color, side, part, half))
+                total = source_cut(color, 0, part)[...] + landing(color, 0, part)[...]
+                picks = [slice(None)] * (dims - 1)
+                result[(color, *picks, strip_rows[part])] = total + landing(color, 1, part)[...]
+
+        return far, close, pass_on, finish
+
+    def nothing(color, j, part):
+        pass
+
+    def direct(color, step, part):
+        at = (me[axes[color][2]] + step) % 4
+        src = sum2.at[color, at, strip_rows[part]]
+        return hop(2, color, step - 1, step, part, src, final3.at[color, step - 1, strip_rows[part]])
+
+    def last_out(part):
+        for step in (2, 1, 3):
+            for color in range(COLORS):
+                direct(color, step, part).start()
+                waiting.append(direct(color, step, part))
+
+    def last_in(part):
         for color in range(COLORS):
-            prepare(color, 2)
-            for side in range(2):
-                away(color, side).start()
-        for color in range(COLORS):
-            for side in range(2):
-                prepare(color, (1, 3)[side])
-                near(color, side, 1 - side).start()
-        for color in range(COLORS):
-            for side in range(2):
-                away(color, side).wait_recv()
-                add(source_cut(color, (1, 3)[side], side), relay.at[color, side])
-                near(color, side, side).start()
-        for color in range(COLORS):
-            prepare(color, 0)
-            for side in range(2):
-                for half in range(2):
-                    near(color, side, half).wait_recv()
-            mine = source_cut(color, 0, None)
-            result[color] = mine[...] + final[color, 0] + final[color, 1]
-        for color in range(COLORS):
-            for side in range(2):
-                waiting.append(away(color, side))
-                for half in range(2):
-                    waiting.append(near(color, side, half))
-
-    def nothing(color, j):
-        pass
-
-    phase(0, own, relay1, final1, sum1, arrived)
-    phase(1, sum1, relay2, final2, sum2, nothing)
-    phase(2, sum2, relay3, final3, sum3, nothing)
+            total = sum2[color, me[axes[color][2]], strip_rows[part]]
+            for step in (1, 3, 2):
+                direct(color, step, part).wait_recv()
+                total = total + final3[color, step - 1, strip_rows[part]]
+            sum3[color, strip_rows[part]] = total
+
+    far1, close1, pass1, finish1 = ring(0, own, relay1, final1, sum1, arrived)
+    far2, close2, pass2, finish2 = ring(1, sum1, relay2, final2, sum2, nothing)
+    far1(0), close1(0), far1(1), pass1(0), close1(1), finish1(0)
+    far2(0), close2(0), pass1(1), pass2(0), finish1(1)
+    far2(1), close2(1), finish2(0), last_out(0), pass2(1), last_in(0)
+    finish2(1), last_out(1), last_in(1)
 
     low_half = r < 8
     group = jnp.where(low_half, r, 15 - r)
@@ -446,9 +559,9 @@
     gather_row(row2, two_recv)
     out_solution[...] = mine + weight[...] * (reduced - total(row2))
 
-    for color in range(COLORS):
-        for j in steps:
-            pairs(color, j).wait_send()
+    for j, part in everything:
+        for color in range(COLORS):
+            pairs(color, j, part).wait_send()
     for copy in waiting:
         copy.wait_send()
     for t in range(17):
@@ -482,28 +595,32 @@
 
 
 def partial_sum(local_inverse, coupling, local_rhs, members):
-    weeks = local_inverse.shape[0]
-    mapped = pltpu.VMEM((HEAD + TOUCHED * BLOCK, LOCAL), bf16)
-    held = pltpu.VMEM((LOCAL, TOUCHED * BLOCK), bf16)
+    def two(rows, columns, dtype=bf16):
+        return (pltpu.VMEM((rows, columns), dtype),) * 2
+
+    columns = TOUCHED * BLOCK
     return pl.pallas_call(
         eliminate,
-        grid_spec=pltpu.PrefetchScalarGridSpec(
-            num_scalar_prefetch=1,
-            grid=(weeks,),
-            in_specs=[
-                pl.BlockSpec((1, LOCAL, LOCAL), lambda w, m: (w, 0, 0)),
-                pl.BlockSpec((1, LOCAL, TOUCHED * BLOCK), lambda w, m: (w, 0, 0)),
-                pl.BlockSpec((1, 1, LOCAL), lambda w, m: (w, 0, 0)),
-            ],
-            out_specs=pl.BlockSpec((GRID, 8, BLOCK), lambda w, m: (0, 0, 0)),
-            scratch_shapes=[mapped, mapped, held, held, mapped, mapped],
-        ),
+        in_specs=[
+            pl.BlockSpec(memory_space=pltpu.SMEM),
+            pl.BlockSpec(memory_space=pltpu.HBM),
+            pl.BlockSpec(memory_space=pltpu.HBM),
+            pl.BlockSpec(memory_space=pltpu.VMEM),
+        ],
+        out_specs=pl.BlockSpec(memory_space=pltpu.VMEM),
+        scratch_shapes=[
+            two(LOCAL, LOCAL, f32),
+            two(LOCAL, columns, f32),
+            pltpu.SemaphoreType.DMA((2, 2)),
+            (two(HEAD + columns, LOCAL),) * 2,
+            (two(LOCAL, columns),) * 2,
+            (two(LOCAL, LOCAL),) * 2,
+            two(HEAD + columns, LOCAL),
+        ],
         out_shape=jax.ShapeDtypeStruct((GRID, 8, BLOCK), f32),
-        compiler_params=pltpu.CompilerParams(
-            dimension_semantics=("arbitrary",), vmem_limit_bytes=60 * 2**20
-        ),
+        compiler_params=pltpu.CompilerParams(vmem_limit_bytes=34 * 2**20),
         name="eliminate",
-    )(members, local_inverse, coupling, local_rhs.reshape(weeks, 1, LOCAL))
+    )(members, local_inverse, coupling, local_rhs)
 
 
 def combined(summed, shared_matrix, shared_rhs, prior_solution, preconditioner):
@@ -533,8 +650,7 @@
             buffer(COLORS, 2, 2, strip, BLOCK),
             buffer(COLORS, 2, 4, strip, BLOCK),
             buffer(COLORS, 4, strip, BLOCK),
-            buffer(COLORS, 2, strip // 2, BLOCK),
-            buffer(COLORS, 2, strip, BLOCK),
+            buffer(COLORS, 3, strip, BLOCK),
             buffer(COLORS, strip, BLOCK),
             buffer(2, 16, 8, BLOCK),
             buffer(8, BLOCK),
@@ -544,11 +660,11 @@
             buffer(8, 8, BLOCK),
             buffer(2, 8, 8, BLOCK),
             buffer(8, 8, BLOCK),
-            dma((COLORS, 4)),
-            dma((COLORS, 4)),
-            dma((COLORS, 4)),
-            dma((3, COLORS, 6)),
-            dma((3, COLORS, 6)),
+            dma((2, COLORS, 4)),
+            dma((2, COLORS, 4)),
+            dma((2, COLORS, 4)),
+            dma((2, 3, COLORS, 6)),
+            dma((2, 3, COLORS, 6)),
             dma((17, 2)),
             dma((2, 16)),
             dma((23,)),
@@ -561,7 +677,7 @@
             dma((8,)),
         ],
         compiler_params=pltpu.CompilerParams(
-            collective_id=0, has_side_effects=True, vmem_limit_bytes=40 * 2**20
+            collective_id=0, has_side_effects=True, vmem_limit_bytes=24 * 2**20
         ),
         name="combine",
     )(

time: 114 us -> 107 us (0.939)
  Pallas kernels: 105 us -> 98.1 us
    pallas_call x1, Pallas kernels: 47.8 us -> 42.5 us  [partial_sum(): pl.pallas_call(eliminate, in_specs=[pl.BlockSpec(memory_space=pltpu.SMEM)...]
    pallas_call x1, Pallas kernels: 57 us -> 55.6 us  [combined(): pl.pallas_call(combine, in_specs=[pl.BlockSpec(memory_space=pl.ANY)] + [v...]
    reshape x1 -> x0, local copies, waits for them, and re-layouts: 1.33 us -> none  [partial_sum(): local_rhs.reshape(weeks, 1, LOCAL)]
    unnamed x13 -> x17, local copies, waits for them, and re-layouts: 5.37 us -> 6.47 us
where the time goes in v2:
time: 107 us; the launch traced here: 105 us
  Pallas kernels  98.1 us (92%)
  local copies, waits for them, and re-layouts  6.47 us (6%)
    pallas_call x1, Pallas kernels, combined(): pl.pallas_call(combine, in_specs=[pl.BlockSpec(memory_space=pl.ANY)] + [v...  55.6 us
    pallas_call x1, Pallas kernels, partial_sum(): pl.pallas_call(eliminate, in_specs=[pl.BlockSpec(memory_space=pltpu.SMEM)...  42.5 us
    unnamed x17, local copies, waits for them, and re-layouts  6.47 us

profile of v2, /device:TPU:40, one launch (start us, length us, event | category | flops | bytes accessed | tf_op | source)
XLA Modules:
  0.0 105.3 jit_solution(4860077826711402177)
XLA Ops:
  0.6 0.0 copy-start
  0.6 3.4 %copy-done = f32[8,512,512]{2,1,0:T(8,128)S(1)} copy-done((f32[8,512,512]{2,1,0:T(8,128)S(1)}, f32[8,512,512]{2,1,0:T(8,128)}, u32[]{:S(2)}) %copy-start) | copy-done | bytes 8388632
  4.0 0.0 copy-start.2
  4.0 0.7 copy-done.2
  4.7 0.0 copy-start.3
  4.7 0.7 copy-done.3
  5.4 0.0 copy-start.1
  5.4 0.0 copy-start.4
  5.4 0.0 copy-start.5
  5.4 0.0 copy-start.6
  5.4 42.5 %eliminate.1 = f32[2304,8,128]{2,1,0:T(8,128)S(1)} custom-call(s32[8,8]{1,0:T(8,128)S(1)} %copy-done.3, f32[8,512,512]{2,1,0:T(8,128)S(1)} %copy-done, f32[8,512,1024]{2,1,0:T(8,128)} %coupling.1, f32[8,512]{1,0:T(8,128)S(1)} %copy-done.2), custom_call_target="tpu_custom_call" | custom-call | tf_op jit(solution)/shard_map/eliminate/pallas_call | solution.py:602
  48.0 0.0 copy-done.1
  48.0 0.0 copy-done.4
  48.0 0.0 copy-done.5
  48.0 0.0 copy-done.6
  48.0 55.6 %combine.1 = (f32[128,256]{1,0:T(8,128)S(1)}, f32[1,128]{1,0:T(1,128)S(1)}, f32[1,128]{1,0:T(1,128)S(1)}) custom-call(f32[3,2,4,4,4,48,128]{6,5,4,3,2,1,0:T(8,128)S(1)} %bitcast.6, f32[128,256]{1,0:T(8,128)S(1)} %copy-done.1, f32[1,128]{1,0:T(1,128)S(1)} %bitcast.7, f32[1,128]{1,0:T(1,128)S(1)} %bitcast.8, f32[1,128]{1,0:T(1,128)S(1)} %bitcast.9), custom_call_target="tpu_custom_call" | custom-call | tf_op jit(solution)/shard_map/combine/pallas_call | solution.py:635
  103.6 0.7 copy.14
  104.3 0.5 copy.15
  104.8 0.5 copy.16
Async XLA Ops:
  0.6 3.4 %copy-start = (f32[8,512,512]{2,1,0:T(8,128)S(1)}, f32[8,512,512]{2,1,0:T(8,128)}, u32[]{:S(2)}) copy-start(f32[8,512,512]{2,1,0:T(8,128)} %inverse.1) | copy-start | bytes 25165828
  4.0 0.7 copy-start.2
  4.7 0.7 copy-start.3
  5.4 42.5 %copy-start.1 = (f32[128,256]{1,0:T(8,128)S(1)}, f32[128,256]{1,0:T(8,128)}, u32[]{:S(2)}) copy-start(f32[128,256]{1,0:T(8,128)} %matrix.1) | copy-start | bytes 393220
  5.4 42.5 %copy-start.4 = (f32[128]{0:T(128)S(1)}, f32[128]{0:T(128)}, u32[]{:S(2)}) copy-start(f32[128]{0:T(128)} %param.13) | copy-start | bytes 1540
  5.4 42.5 %copy-start.5 = (f32[128]{0:T(128)S(1)}, f32[128]{0:T(128)}, u32[]{:S(2)}) copy-start(f32[128]{0:T(128)} %param.14) | copy-start | bytes 1540
  5.4 42.6 %copy-start.6 = (f32[128]{0:T(128)S(1)}, f32[128]{0:T(128)}, u32[]{:S(2)}) copy-start(f32[128]{0:T(128)} %param.15) | copy-start | bytes 1540
